TPU v7x, 32 devices: a whole 2x2x4 slice. The times are simulated.
32 devices in a mesh: band: 8 (over y, x, core), gblk: 4 (over z).
Axes of the slice: x: 2, y: 2, z: 4, core: 2. Of those that a mesh axis runs over, the one named last changes fastest.
Arguments:
- eps_inv: bfloat16 [2, 2, 8, 4, 512, 16384], P(None, None, None, 'gblk', None, 'band'), may hold values from -6 to 6
- pair_elements: bfloat16 [2, 1, 16, 16384], P(None, None, 'band'), may hold values from -0.046875 to 0.046875
Outputs:
- sigma_terms: float32 [2, 2, 1, 16], P(None, None, None, 'band')
All inputs are finite; a program needn't handle non-finite values.
Results may differ from a plain program's by a relative error of at most 0.0003.
Values may be sent and summed in bfloat16 or wider, within the bound.
No kernel may reach another device: no remote copies, remote signals or barrier semaphores. Data moves between devices by JAX's collectives and lax.ppermute only.
A program may use at most 128 MiB of HBM per device.

v0:
```python
import jax
import jax.numpy as jnp
from jax import lax
from jax.sharding import PartitionSpec as P


def shards(eps_inv, pair_elements):
    group_count = lax.axis_size("gblk")
    group_index = lax.axis_index("gblk")
    freqs = eps_inv.shape[0]
    rounds = eps_inv.shape[2]
    tile_rows = eps_inv.shape[4]
    width = eps_inv.shape[5]
    states = pair_elements.shape[1]
    local_bands = pair_elements.shape[2]
    columns = lax.all_to_all(pair_elements, "band", split_axis=3, concat_axis=2, tiled=True)
    all_bands = columns.shape[2]
    blocks = eps_inv.reshape(freqs, 2, -1, width)
    shaped = pair_elements.reshape(2, states, local_bands, rounds, group_count, tile_rows)
    picked = lax.dynamic_slice_in_dim(shaped, group_index, 1, 4)
    row_local = picked.reshape(2, states, local_bands, rounds * tile_rows)
    flat = columns.reshape(-1, width)
    contract_last = (((1,), (1,)), ((), ()))
    images = []
    for frequency in range(freqs):
        along_a = lax.dot_general(
            flat, blocks[frequency, 0], contract_last, preferred_element_type=jnp.float32
        )
        along_b = lax.dot_general(
            flat, blocks[frequency, 1], contract_last, preferred_element_type=jnp.float32
        )
        along_a = along_a.reshape(2, states, all_bands, -1)
        along_b = along_b.reshape(2, states, all_bands, -1)
        images.append(jnp.stack([along_a[0] - along_b[1], along_a[1] + along_b[0]]))
    image = jnp.stack(images)
    piece = lax.all_gather(row_local, "band", axis=2, tiled=True)
    real_part = piece[0].astype(jnp.float32)
    imag_part = piece[1].astype(jnp.float32)
    sigma_re = jnp.sum(real_part * image[:, 0] + imag_part * image[:, 1], axis=-1)
    sigma_im = jnp.sum(real_part * image[:, 1] - imag_part * image[:, 0], axis=-1)
    partial_sigma = jnp.stack([sigma_re, sigma_im], axis=1)
    reduced = lax.psum_scatter(partial_sigma, "band", scatter_dimension=3, tiled=True)
    return lax.psum(reduced, "gblk")


def solution(mesh):
    placed = (P(None, None, None, "gblk", None, "band"), P(None, None, "band", None))
    return jax.shard_map(
        shards, mesh=mesh, in_specs=placed, out_specs=P(None, None, None, "band"), check_vma=False
    )
```

profile of v0, /device:TPU:0, one launch (start us, length us, event | category | flops | bytes accessed | tf_op | source)
XLA Modules:
  0.0 138.5 jit_solution(16395664978475546550)
XLA Ops:
  0.0 15.4 %copy.24 = bf16[2,1,2,16384]{2,0,1,3:T(2,128)(2,1)} copy(bf16[2,1,2,16384]{3,2,1,0:T(2,128)(2,1)} %param.3) | data formatting | bytes 262144 | tf_op args[1]
  15.5 13.7 %reshape.124 = bf16[8,2,4096]{2,1,0:T(2,128)(2,1)} reshape(bf16[16384,1,2,2]{3,2,1,0:T(2,128)(2,1)} %bitcast.63) | data formatting | bytes 262144
  29.2 5.2 %all-to-all-start = ((bf16[8,2,4096]{2,1,0:T(2,128)(2,1)}), bf16[8,2,4096]{2,1,0:T(2,128)(2,1)S(1)}, u32[]{:S(2)}, u32[]{:S(2)}) async-start(bf16[8,2,4096]{2,1,0:T(2,128)(2,1)} %reshape.124), calls=%async_computation | async-start | bytes 262144 | tf_op jit(solution)/shard_map/all_to_all | solution.py:16
  34.4 0.1 reshape.113
  34.5 0.2 dynamic-slice_reduce_fusion
  34.8 9.8 %all_gather.3 = bf16[2,1,16,4096]{3,0,1,2:T(2,128)(2,1)S(1)} all-gather(bf16[2,1,2,4096]{3,0,1,2:T(2,128)(2,1)S(1)} %copy.23), channel_id=1, replica_groups=mesh['band'=8,'gblk'=4] {'band'}, dimensions={2}, use_global_device_ids=true | all-gather | bytes 294912 | tf_op jit(solution)/shard_map/all_gather | solution.py:36
  44.6 0.5 slice_convert_fusion.1
  45.1 0.3 copy_bitcast_fusion
  45.4 0.6 dynamic-slice
  46.7 19.1 %reshape.125 = bf16[16384,1,2,2]{3,2,1,0:T(2,128)(2,1)} reshape(bf16[8,2,4096]{2,1,0:T(2,128)(2,1)S(1)} %all-to-all-done) | data formatting | bytes 262144
  65.8 11.9 %copy.29 = bf16[2,1,2,8,2048]{4,3,2,0,1:T(8,128)(2,1)S(1)} copy(bf16[2,1,2,8,2048]{2,0,4,3,1:T(2,128)(2,1)} %bitcast.62) | data formatting | bytes 262144 | tf_op jit(solution)/shard_map/all_to_all | solution.py:16
  77.6 0.1 copy.26
  77.8 0.1 reshape.115
  77.9 8.6 %fusion.2 = f32[32,4096]{1,0:T(8,128)S(1)} fusion(bf16[32,2048]{1,0:T(8,128)(2,1)S(1)} %reshape.115, bf16[2,2,4096,2048]{3,2,1,0:T(8,128)(2,1)} %bitcast.2), kind=kOutput, calls=%fused_computation.5 | convolution fusion | flops 536870912 | bytes 17432576 | tf_op jit(solution)/shard_map/dot_general | solution.py:29
  86.4 8.6 %fusion.3 = f32[32,4096]{1,0:T(8,128)S(1)} fusion(bf16[32,2048]{1,0:T(8,128)(2,1)S(1)} %reshape.115, bf16[2,2,4096,2048]{3,2,1,0:T(8,128)(2,1)} %bitcast.2), kind=kOutput, calls=%fused_computation.7 | convolution fusion | flops 536870912 | bytes 17432576 | tf_op jit(solution)/shard_map/dot_general | solution.py:26
  95.0 8.6 %fusion = f32[32,4096]{1,0:T(8,128)S(1)} fusion(bf16[32,2048]{1,0:T(8,128)(2,1)S(1)} %reshape.115, bf16[2,2,4096,2048]{3,2,1,0:T(8,128)(2,1)} %bitcast.2), kind=kOutput, calls=%fused_computation.1 | convolution fusion | flops 536870912 | bytes 17432576 | tf_op jit(solution)/shard_map/dot_general | solution.py:29
  103.6 8.6 %fusion.1 = f32[32,4096]{1,0:T(8,128)S(1)} fusion(bf16[32,2048]{1,0:T(8,128)(2,1)S(1)} %reshape.115, bf16[2,2,4096,2048]{3,2,1,0:T(8,128)(2,1)} %bitcast.2), kind=kOutput, calls=%fused_computation.3 | convolution fusion | flops 536870912 | bytes 17432576 | tf_op jit(solution)/shard_map/dot_general | solution.py:26
  112.2 0.1 fusion.10
  112.3 0.1 fusion.8
  112.4 0.2 add_reduce_fusion
  112.7 13.2 %all-reduce = f32[2,2,1,16]{3,0,2,1:T(2,128)S(1)} all-reduce(f32[2,2,1,16]{3,0,2,1:T(2,128)S(1)} %pad_maximum_fusion.1), channel_id=2, replica_groups=mesh['band'=8,'gblk'=4] {'band'}, use_global_device_ids=true, to_apply=%region_2.0.clone | all-reduce | flops 64 | bytes 512
  125.9 0.1 constant_dynamic-slice_fusion
  125.9 11.9 %psum.7 = f32[2,2,1,2]{3,0,2,1:T(2,128)S(1)} all-reduce(f32[2,2,1,2]{3,0,2,1:T(2,128)S(1)} %constant_dynamic-slice_fusion), channel_id=1, replica_groups=mesh['band'=8,'gblk'=4] {'gblk'}, use_global_device_ids=true, to_apply=%region_3.0 | all-reduce | flops 8 | bytes 64 | tf_op jit(solution)/shard_map/psum | solution.py:43
  137.9 0.6 copy.28
  (10 shorter events, 0.1 us)
Async XLA Ops:
  0.0 45.4 %copy-start.1 = (u32[32]{0:T(128)S(1)}, u32[32]{0:T(128)}, u32[]{:S(2)}) copy-start(u32[32]{0:T(128)} %constant.14) | copy-start | bytes 388
  0.0 34.4 %copy-start = (bf16[2,1,2,16384]{3,2,1,0:T(2,128)(2,1)S(1)}, bf16[2,1,2,16384]{3,2,1,0:T(2,128)(2,1)}, u32[]{:S(2)}) copy-start(bf16[2,1,2,16384]{3,2,1,0:T(2,128)(2,1)} %param.3) | copy-start | bytes 393220
  29.2 17.5 %all-to-all-start = ((bf16[8,2,4096]{2,1,0:T(2,128)(2,1)}), bf16[8,2,4096]{2,1,0:T(2,128)(2,1)S(1)}, u32[]{:S(2)}, u32[]{:S(2)}) async-start(bf16[8,2,4096]{2,1,0:T(2,128)(2,1)} %reshape.124), calls=%async_computation | async-start | bytes 262144 | tf_op jit(solution)/shard_map/all_to_all | solution.py:16
where the time goes:
time: 140 us; the launch traced here: 138 us
  local copies, waits for them, and re-layouts  62.2 us (44%)
  blocking collectives  35 us (25%)
  matrix products  34.3 us (24%)
  starting transfers between devices  5.2 us (4%)
    unnamed x10, local copies, waits for them, and re-layouts  49.2 us
    dot_general x2, matrix products, shards(): lax.dot_general(flat, blocks[frequency, 0], contract_last, preferred_elem...  17.2 us
    dot_general x2, matrix products, shards(): lax.dot_general(flat, blocks[frequency, 1], contract_last, preferred_elem...  17.1 us
    unnamed x1, blocking collectives  13.2 us
    all_to_all x2, local copies, waits for them, and re-layouts, shards(): lax.all_to_all(pair_elements, 'band', split_axis=3, concat_axis=2, tiled=...  12 us
    psum x1, blocking collectives, shards(): return lax.psum(reduced, 'gblk')  11.9 us
    all_gather x1, blocking collectives, shards(): piece = lax.all_gather(row_local, 'band', axis=2, tiled=True)  9.81 us
    all_to_all x1, starting transfers between devices, shards(): lax.all_to_all(pair_elements, 'band', split_axis=3, concat_axis=2, tiled=...  5.2 us
  transfers between devices with their start and end apart: 1, of which 0 were waited for; matrix products, arithmetic and copies ran while one was open for 1% of the time, Pallas kernels for 0%

commit v1 on v0

--- a/solution.py
+++ b/solution.py
@@ -13,7 +13,11 @@
     width = eps_inv.shape[5]
     states = pair_elements.shape[1]
     local_bands = pair_elements.shape[2]
-    columns = lax.all_to_all(pair_elements, "band", split_axis=3, concat_axis=2, tiled=True)
+    raw_out = lax.psum(1, axis_name="band")
+    x_new = jnp.split(pair_elements, raw_out, 3)
+    item_now = jnp.stack(x_new)
+    val2 = lax.all_to_all(item_now, axis_name="band", split_axis=0, concat_axis=0)
+    columns = jnp.concatenate(val2, 2)
     all_bands = columns.shape[2]
     blocks = eps_inv.reshape(freqs, 2, -1, width)
     shaped = pair_elements.reshape(2, states, local_bands, rounds, group_count, tile_rows)

time: 140 us -> 91.2 us (0.65)
  local copies, waits for them, and re-layouts: 62.2 us -> 14.2 us
    unnamed x10, local copies, waits for them, and re-layouts: 49.2 us -> 10.9 us
    all_to_all x2 -> x0, local copies, waits for them, and re-layouts: 12 us -> none  [shards(): lax.all_to_all(pair_elements, 'band', split_axis=3, concat_axis=2, tiled=...]
  transfers between devices with their start and end apart: 1 -> 1, of which waited for: 0 -> 0; matrix products, arithmetic and copies ran while one was open for 1% -> 4% of each run, Pallas kernels for 0% -> 0%
where the time goes in v1:
time: 91.2 us; the launch traced here: 90.4 us
  blocking collectives  35 us (38%)
  matrix products  34.3 us (38%)
  local copies, waits for them, and re-layouts  14.2 us (16%)
  starting transfers between devices  5.2 us (6%)
  other arithmetic  1.01 us (1%)
    dot_general x2, matrix products, shards(): lax.dot_general(flat, blocks[frequency, 0], contract_last, preferred_elem...  17.2 us
    dot_general x2, matrix products, shards(): lax.dot_general(flat, blocks[frequency, 1], contract_last, preferred_elem...  17.1 us
    unnamed x1, blocking collectives  13.2 us
    psum x1, blocking collectives, shards(): return lax.psum(reduced, 'gblk')  11.9 us
    unnamed x10, local copies, waits for them, and re-layouts  10.9 us
    all_gather x1, blocking collectives, shards(): piece = lax.all_gather(row_local, 'band', axis=2, tiled=True)  9.81 us
    all_to_all x1, starting transfers between devices, shards(): lax.all_to_all(item_now, axis_name='band', split_axis=0, concat_axis=0)  5.2 us
  transfers between devices with their start and end apart: 1, of which 0 were waited for; matrix products, arithmetic and copies ran while one was open for 4% of the time, Pallas kernels for 0%

profile of v1, /device:TPU:0, one launch (start us, length us, event | category | flops | bytes accessed | tf_op | source)
XLA Modules:
  0.0 90.4 jit_solution(16909850481913745224)
XLA Ops:
  0.0 1.3 %constant_dynamic-update-slice_fusion.7 = bf16[8,2,1,2,2048]{4,3,1,2,0:T(2,128)(2,1)} fusion(bf16[2,1,2,16384]{3,2,0,1:T(2,128)(2,1)} %bitcast.96), kind=kLoop, calls=%fused_computation.38 | loop fusion | bytes 32768
  1.3 1.3 %constant_dynamic-update-slice_fusion.6 = bf16[8,2,1,2,2048]{4,3,1,2,0:T(2,128)(2,1)} fusion(bf16[8,2,1,2,2048]{4,3,1,2,0:T(2,128)(2,1)} %constant_dynamic-update-slice_fusion.7, bf16[2,1,2,16384]{3,2,0,1:T(2,128)(2,1)} %bitcast.97), kind=kLoop, calls=%fused_computation.37 | loop fusion | bytes 32768
  2.7 1.3 %constant_dynamic-update-slice_fusion.5 = bf16[8,2,1,2,2048]{4,3,1,2,0:T(2,128)(2,1)} fusion(bf16[8,2,1,2,2048]{4,3,1,2,0:T(2,128)(2,1)} %constant_dynamic-update-slice_fusion.6, bf16[2,1,2,16384]{3,2,0,1:T(2,128)(2,1)} %bitcast.98), kind=kLoop, calls=%fused_computation.36 | loop fusion | bytes 32768
  4.0 1.3 %constant_dynamic-update-slice_fusion.4 = bf16[8,2,1,2,2048]{4,3,1,2,0:T(2,128)(2,1)} fusion(bf16[8,2,1,2,2048]{4,3,1,2,0:T(2,128)(2,1)} %constant_dynamic-update-slice_fusion.5, bf16[2,1,2,16384]{3,2,0,1:T(2,128)(2,1)} %bitcast.99), kind=kLoop, calls=%fused_computation.35 | loop fusion | bytes 32768
  5.3 1.3 %constant_dynamic-update-slice_fusion.3 = bf16[8,2,1,2,2048]{4,3,1,2,0:T(2,128)(2,1)} fusion(bf16[8,2,1,2,2048]{4,3,1,2,0:T(2,128)(2,1)} %constant_dynamic-update-slice_fusion.4, bf16[2,1,2,16384]{3,2,0,1:T(2,128)(2,1)} %bitcast.100), kind=kLoop, calls=%fused_computation.34 | loop fusion | bytes 32768
  6.6 1.3 %constant_dynamic-update-slice_fusion.2 = bf16[8,2,1,2,2048]{4,3,1,2,0:T(2,128)(2,1)} fusion(bf16[8,2,1,2,2048]{4,3,1,2,0:T(2,128)(2,1)} %constant_dynamic-update-slice_fusion.3, bf16[2,1,2,16384]{3,2,1,0:T(2,128)(2,1)} %param.3), kind=kLoop, calls=%fused_computation.33 | loop fusion | bytes 32768
  8.0 1.3 %constant_dynamic-update-slice_fusion.1 = bf16[8,2,1,2,2048]{4,3,1,2,0:T(2,128)(2,1)} fusion(bf16[8,2,1,2,2048]{4,3,1,2,0:T(2,128)(2,1)} %constant_dynamic-update-slice_fusion.2, bf16[2,1,2,16384]{3,2,0,1:T(2,128)(2,1)} %bitcast.101), kind=kLoop, calls=%fused_computation.32 | loop fusion | bytes 32768
  9.3 1.3 %constant_dynamic-update-slice_fusion = bf16[8,2,1,2,2048]{4,3,1,2,0:T(2,128)(2,1)} fusion(bf16[8,2,1,2,2048]{4,3,1,2,0:T(2,128)(2,1)} %constant_dynamic-update-slice_fusion.1, bf16[2,1,2,16384]{3,2,0,1:T(2,128)(2,1)} %bitcast.102), kind=kLoop, calls=%fused_computation.31 | loop fusion | bytes 32768 | tf_op jit(solution)/shard_map/stack | solution.py:18
  10.6 5.2 %all-to-all-start = ((bf16[8,2,1,2,2048]{4,3,1,2,0:T(2,128)(2,1)}), bf16[8,2,1,2,2048]{4,3,1,2,0:T(2,128)(2,1)S(1)}, u32[]{:S(2)}, u32[]{:S(2)}) async-start(bf16[8,2,1,2,2048]{4,3,1,2,0:T(2,128)(2,1)} %constant_dynamic-update-slice_fusion), calls=%async_computation | async-start | bytes 262144 | tf_op jit(solution)/shard_map/all_to_all | solution.py:19
  15.8 1.0 %reshape.112 = bf16[2,1,2,8,4,512]{5,4,3,2,0,1:T(4,128)(2,1)S(1)} reshape(bf16[2,1,2,16384]{3,2,1,0:T(2,128)(2,1)} %param.3) | data formatting | bytes 262144 | tf_op jit(solution)/shard_map/reshape | solution.py:23
  16.8 0.2 dynamic-slice_reduce_fusion
  17.1 9.8 %all_gather.3 = bf16[2,1,16,4096]{3,0,1,2:T(2,128)(2,1)S(1)} all-gather(bf16[2,1,2,4096]{3,0,1,2:T(2,128)(2,1)S(1)} %copy.24), channel_id=1, replica_groups=mesh['band'=8,'gblk'=4] {'band'}, dimensions={2}, use_global_device_ids=true | all-gather | bytes 294912 | tf_op jit(solution)/shard_map/all_gather | solution.py:40
  26.9 0.5 slice_convert_fusion.1
  27.5 0.3 copy_bitcast_fusion
  27.8 1.2 %dynamic-slice = u32[1]{0:T(128)} dynamic-slice(u32[32]{0:T(128)} %constant.14, u32[]{:T(128)S(6)} %add.31), dynamic_slice_sizes={1} | dynamic-slice | bytes 12
  29.8 8.6 %fusion.2 = f32[32,4096]{1,0:T(8,128)S(1)} fusion(bf16[32,2048]{1,0:T(8,128)(2,1)S(1)} %reshape_reshape.3, bf16[2,2,4096,2048]{3,2,1,0:T(8,128)(2,1)} %bitcast.16), kind=kOutput, calls=%fused_computation.5 | convolution fusion | flops 536870912 | bytes 17432576 | tf_op jit(solution)/shard_map/dot_general | solution.py:33
  38.4 8.6 %fusion.3 = f32[32,4096]{1,0:T(8,128)S(1)} fusion(bf16[32,2048]{1,0:T(8,128)(2,1)S(1)} %reshape_reshape.3, bf16[2,2,4096,2048]{3,2,1,0:T(8,128)(2,1)} %bitcast.16), kind=kOutput, calls=%fused_computation.7 | convolution fusion | flops 536870912 | bytes 17432576 | tf_op jit(solution)/shard_map/dot_general | solution.py:30
  47.0 8.6 %fusion = f32[32,4096]{1,0:T(8,128)S(1)} fusion(bf16[32,2048]{1,0:T(8,128)(2,1)S(1)} %reshape_reshape.3, bf16[2,2,4096,2048]{3,2,1,0:T(8,128)(2,1)} %bitcast.16), kind=kOutput, calls=%fused_computation.1 | convolution fusion | flops 536870912 | bytes 17432576 | tf_op jit(solution)/shard_map/dot_general | solution.py:33
  55.6 8.6 %fusion.1 = f32[32,4096]{1,0:T(8,128)S(1)} fusion(bf16[32,2048]{1,0:T(8,128)(2,1)S(1)} %reshape_reshape.3, bf16[2,2,4096,2048]{3,2,1,0:T(8,128)(2,1)} %bitcast.16), kind=kOutput, calls=%fused_computation.3 | convolution fusion | flops 536870912 | bytes 17432576 | tf_op jit(solution)/shard_map/dot_general | solution.py:30
  64.1 0.1 fusion.10
  64.4 0.2 add_reduce_fusion
  64.6 13.2 %all-reduce = f32[2,2,1,16]{3,0,2,1:T(2,128)S(1)} all-reduce(f32[2,2,1,16]{3,0,2,1:T(2,128)S(1)} %pad_maximum_fusion.1), channel_id=2, replica_groups=mesh['band'=8,'gblk'=4] {'band'}, use_global_device_ids=true, to_apply=%region_2.0.clone | all-reduce | flops 64 | bytes 512
  77.9 11.9 %psum.7 = f32[2,2,1,2]{3,0,2,1:T(2,128)S(1)} all-reduce(f32[2,2,1,2]{3,0,2,1:T(2,128)S(1)} %constant_dynamic-slice_fusion), channel_id=1, replica_groups=mesh['band'=8,'gblk'=4] {'gblk'}, use_global_device_ids=true, to_apply=%region_3.0 | all-reduce | flops 8 | bytes 64 | tf_op jit(solution)/shard_map/psum | solution.py:47
  89.9 0.6 copy.34
  (10 shorter events, 0.4 us)
Async XLA Ops:
  10.6 19.1 %all-to-all-start = ((bf16[8,2,1,2,2048]{4,3,1,2,0:T(2,128)(2,1)}), bf16[8,2,1,2,2048]{4,3,1,2,0:T(2,128)(2,1)S(1)}, u32[]{:S(2)}, u32[]{:S(2)}) async-start(bf16[8,2,1,2,2048]{4,3,1,2,0:T(2,128)(2,1)} %constant_dynamic-update-slice_fusion), calls=%async_computation | async-start | bytes 262144 | tf_op jit(solution)/shard_map/all_to_all | solution.py:19
